TPU v7x, 64 devices: a 2x2x8 block of a 4x4x8 slice. The times are simulated.
64 devices in a mesh: batch: 4 (over x, y), graph: 16 (over z, core).
Axes of the slice: x: 2, y: 2, z: 8, core: 2. Of those that a mesh axis runs over, the one named last changes fastest.
The devices are a block of a 4x4x8 slice.
Arguments:
- features: bfloat16 [131072, 500], P(('batch', 'graph')), parts along dimension 0
- w_msg1: bfloat16 [500, 256], replicated
- w_self1: bfloat16 [500, 256], replicated
- w_msg2: bfloat16 [256, 256], replicated
- w_self2: bfloat16 [256, 256], replicated
- src_local: int32 [64, 20480], P(('batch', 'graph')), parts along dimension 0
- send_slot: int32 [64, 20480], P(('batch', 'graph')), parts along dimension 0
- edge_weight: float32 [64, 20480], P(('batch', 'graph')), parts along dimension 0
- recv_row: int32 [64, 16, 512], P(('batch', 'graph')), parts along dimension 0
Outputs:
- output: bfloat16 [131072, 256], P(('batch', 'graph')), parts along dimension 0
There are 4 independent parts. A program takes and returns all parts, laid end to end along the dimension named above; an argument that names none is the same for every part.
All inputs are finite; a program needn't handle non-finite values.
Results may differ from a plain program's by a relative error of at most 0.00844026.
Values are sent between devices in bfloat16 or wider.
A program may use at most 768 MiB of HBM per device.

v0:
```python
import jax
import jax.numpy as jnp
from jax import lax
from jax.sharding import PartitionSpec as P


def solution(mesh):
    row_spec = P(("batch", "graph"), None)
    full_spec = P(None, None)
    table_spec = P(("batch", "graph"), None, None)

    def gnn_layer(h_loc, w_msg, w_self, src_idx, slot_idx, edge_w, recv_idx):
        rows_dev = h_loc.shape[0]
        messages = jnp.dot(h_loc, w_msg, preferred_element_type=jnp.float32).astype(jnp.bfloat16)
        weighted = messages[src_idx].astype(jnp.float32) * edge_w
        partial = jax.ops.segment_sum(weighted, slot_idx, num_segments=recv_idx.shape[0]).astype(jnp.bfloat16)
        received = lax.all_to_all(partial, "graph", 0, 0, tiled=True)
        agg_sum = jax.ops.segment_sum(received.astype(jnp.float32), recv_idx, num_segments=rows_dev + 1)
        self_term = jnp.dot(h_loc, w_self, preferred_element_type=jnp.float32)
        return jax.nn.relu(self_term + agg_sum[:rows_dev]).astype(jnp.bfloat16)

    def local_step(features, w_msg1, w_self1, w_msg2, w_self2, src_local, send_slot, edge_weight, recv_row):
        src_idx = src_local[0]
        slot_idx = send_slot[0]
        edge_w = edge_weight[0][:, None]
        recv_idx = recv_row[0].reshape(-1)
        hidden1 = gnn_layer(features, w_msg1, w_self1, src_idx, slot_idx, edge_w, recv_idx)
        return gnn_layer(hidden1, w_msg2, w_self2, src_idx, slot_idx, edge_w, recv_idx)

    return jax.shard_map(local_step, mesh=mesh, in_specs=(row_spec, full_spec, full_spec, full_spec, full_spec, row_spec, row_spec, row_spec, table_spec), out_specs=row_spec, check_vma=False)
```

profile of v0, /device:TPU:31, one launch (start us, length us, event | category | flops | bytes accessed | tf_op | source)
XLA Modules:
  0.0 705.8 jit_solution(8411750289157656960)
XLA Ops:
  0.0 0.0 copy-start
  0.0 1.1 compare_select_fusion
  1.1 0.5 copy-done
  1.6 1.8 convolution_convert_fusion
  3.4 187.6 %scatter_custom_fusion = f32[8192,256]{1,0:T(8,128)} fusion(s32[20480]{0:T(1024)} %bitcast.30, f32[20480]{0:T(1024)} %bitcast.24, f32[]{:T(128)} %constant.3.clone.1, bf16[2048,256]{1,0:T(8,128)(2,1)S(1)} %convolution_convert_fusion, s32[20480]{0:T(1024)S(1)} %broadcast_clamp_fusion), kind=kCustom, calls=%fused_computation.9 | custom fusion | flops 15728640 | bytes 9601536 | tf_op jit(solution)/shard_map/scatter-add | solution.py:16
  191.0 5.8 convert_element_type.38
  196.8 10.0 %all-to-all-start = ((bf16[16,512,256]{2,1,0:T(8,128)(2,1)}), bf16[16,512,256]{2,1,0:T(8,128)(2,1)}, u32[]{:S(2)}, u32[]{:S(2)}) async-start(bf16[16,512,256]{2,1,0:T(8,128)(2,1)} %bitcast.21), calls=%async_computation | async-start | bytes 8388608 | tf_op jit(solution)/shard_map/all_to_all | solution.py:17
  206.8 0.0 copy-done.6
  206.8 92.7 %all-to-all-done = bf16[16,512,256]{2,1,0:T(8,128)(2,1)} async-done(((bf16[16,512,256]{2,1,0:T(8,128)(2,1)}), bf16[16,512,256]{2,1,0:T(8,128)(2,1)}, u32[]{:S(2)}, u32[]{:S(2)}) %all-to-all-start) | async-done | bytes 4194336 | tf_op jit(solution)/shard_map/all_to_all | solution.py:17
  299.6 51.0 %scatter_custom_fusion.1 = f32[2049,256]{1,0:T(8,128)} fusion(s32[8192]{0:T(1024)S(1)} %bitcast.28, bf16[8192,256]{1,0:T(8,128)(2,1)} %bitcast.8, f32[]{:T(128)} %constant.3.clone.1), kind=kCustom, calls=%fused_computation.16 | custom fusion | flops 4194304 | bytes 6292484 | tf_op jit(solution)/shard_map/scatter-add | solution.py:18
  350.6 0.0 copy-done.7
  350.6 2.4 fusion.17
  353.0 0.0 copy-start.1
  353.1 1.0 copy-done.1
  354.0 0.0 copy-done.4
  354.0 0.4 convolution_convert_fusion.1
  354.5 188.1 %scatter_custom_fusion.2 = f32[8192,256]{1,0:T(8,128)} fusion(s32[20480]{0:T(1024)} %bitcast.31, f32[20480]{0:T(1024)S(1)} %bitcast.25, f32[]{:T(128)} %constant.3.clone.1, bf16[2048,256]{1,0:T(8,128)(2,1)S(1)} %convolution_convert_fusion.1, s32[20480]{0:T(1024)S(1)} %broadcast_clamp_fusion), kind=kCustom, calls=%fused_computation.6 | custom fusion | flops 15728640 | bytes 9601536 | tf_op jit(solution)/shard_map/scatter-add | solution.py:16
  542.6 3.8 convert_element_type.44
  546.4 0.0 copy-start.2
  546.4 0.0 copy-start.5
  546.4 105.4 %all_to_all.18 = bf16[16,512,256]{2,1,0:T(8,128)(2,1)} all-to-all(bf16[16,512,256]{2,1,0:T(8,128)(2,1)S(1)} %bitcast.22), channel_id=1, replica_groups=mesh['batch'=4,'graph'=16] {'graph'}, dimensions={0} | all-to-all | bytes 8388608 | tf_op jit(solution)/shard_map/all_to_all | solution.py:17
  651.8 51.0 %scatter_custom_fusion.3 = f32[2049,256]{1,0:T(8,128)} fusion(s32[8192]{0:T(1024)S(1)} %bitcast.29, bf16[8192,256]{1,0:T(8,128)(2,1)} %bitcast.23, f32[]{:T(128)} %constant.3.clone.1), kind=kCustom, calls=%fused_computation.14 | custom fusion | flops 4194304 | bytes 6292484 | tf_op jit(solution)/shard_map/scatter-add | solution.py:18
  702.8 0.0 copy-done.2
  702.8 3.0 fusion.16
  (8 shorter events, 0.0 us)
Async XLA Ops:
  0.0 1.6 copy-start
  191.0 15.8 %copy-start.6 = (s32[1,16,512]{2,1,0:T(8,128)S(1)}, s32[1,16,512]{2,1,0:T(8,128)}, u32[]{:S(2)}) copy-start(s32[1,16,512]{2,1,0:T(8,128)} %param.17) | copy-start | bytes 98308
  196.8 153.8 %copy-start.7 = (bf16[500,256]{1,0:T(8,128)(2,1)S(1)}, bf16[500,256]{1,0:T(8,128)(2,1)}, u32[]{:S(2)}) copy-start(bf16[500,256]{1,0:T(8,128)(2,1)} %param.11) | copy-start | bytes 768004
  196.8 157.2 %copy-start.4 = (bf16[256,256]{1,0:T(8,128)(2,1)S(1)}, bf16[256,256]{1,0:T(8,128)(2,1)}, u32[]{:S(2)}) copy-start(bf16[256,256]{1,0:T(8,128)(2,1)} %param.12) | copy-start | bytes 393220
  196.8 102.8 %all-to-all-start = ((bf16[16,512,256]{2,1,0:T(8,128)(2,1)}), bf16[16,512,256]{2,1,0:T(8,128)(2,1)}, u32[]{:S(2)}, u32[]{:S(2)}) async-start(bf16[16,512,256]{2,1,0:T(8,128)(2,1)} %bitcast.21), calls=%async_computation | async-start | bytes 8388608 | tf_op jit(solution)/shard_map/all_to_all | solution.py:17
  206.8 147.6 %copy-start.3 = (f32[1,20480]{1,0:T(1,128)S(1)}, f32[1,20480]{1,0:T(1,128)}, u32[]{:S(2)}) copy-start(f32[1,20480]{1,0:T(1,128)} %param.16) | copy-start | bytes 245764
  353.0 1.0 copy-start.1
  546.4 156.4 %copy-start.2 = (bf16[2048,256]{1,0:T(8,128)(2,1)S(1)}, bf16[2048,256]{1,0:T(8,128)(2,1)}, u32[]{:S(2)}) copy-start(bf16[2048,256]{1,0:T(8,128)(2,1)} %copy-done.1) | copy-start | bytes 3145732
  546.4 156.4 %copy-start.5 = (bf16[256,256]{1,0:T(8,128)(2,1)S(1)}, bf16[256,256]{1,0:T(8,128)(2,1)}, u32[]{:S(2)}) copy-start(bf16[256,256]{1,0:T(8,128)(2,1)} %param.13) | copy-start | bytes 393220
where the time goes:
time: 710 us; the launch traced here: 706 us
  other arithmetic  488 us (69%)
  blocking collectives  105 us (15%)
  waiting for transfers between devices  92.7 us (13%)
  starting transfers between devices  10 us (1%)
  matrix products  7.61 us (1%)
    scatter-add x2, other arithmetic, gnn_layer(): jax.ops.segment_sum(weighted, slot_idx, num_segments=recv_idx.shape[0])  376 us
    all_to_all x1, blocking collectives, gnn_layer(): received = lax.all_to_all(partial, 'graph', 0, 0, tiled=True)  105 us
    scatter-add x2, other arithmetic, gnn_layer(): jax.ops.segment_sum(received.astype(jnp.float32), recv_idx, num_segments=...  102 us
    all_to_all x1, waiting for transfers between devices, gnn_layer(): received = lax.all_to_all(partial, 'graph', 0, 0, tiled=True)  92.7 us
  transfers between devices with their start and end apart: 1, of which 1 were waited for; matrix products, arithmetic and copies ran while one was open for 0% of the time, Pallas kernels for 0%

commit v1 on v0

v1 whole, which is shorter than its diff:
```python
import functools

import jax
import jax.numpy as jnp
from jax import lax
from jax.experimental import pallas as pl
from jax.experimental.pallas import tpu as pltpu
from jax.sharding import PartitionSpec as P

MESH_ID = pl.DeviceIdType.MESH
BF16, F32, I32 = jnp.bfloat16, jnp.float32, jnp.int32
LANES = 128
PAIR_ROWS = 6
SELF_TILE = 256
ROW_CHUNK = 512
NT = (((1,), (1,)), ((), ()))


def dot(a, b):
    return jnp.dot(a, b, preferred_element_type=F32)


def dot_nt(a, b):
    return lax.dot_general(a, b, NT, preferred_element_type=F32)


def one_hot(count, index_row):
    rows = lax.broadcasted_iota(I32, (count, index_row.shape[1]), 0)
    return jnp.where(rows == index_row, 1.0, 0.0).astype(BF16)


def three_pieces(x):
    high = x.astype(BF16)
    rest = x - high.astype(F32)
    mid = rest.astype(BF16)
    low = (rest - mid.astype(F32)).astype(BF16)
    return high, mid, low


def weighted_sum(values, index_row, count):
    select = one_hot(count, index_row)
    high, mid, low = three_pieces(values)
    return dot_nt(high, select) + dot_nt(mid, select) + dot_nt(low, select)


def prep_kernel(peers, slot_cap, rows_dev, cap, start_ref, flag_ref, key_ref, w_ref, src_ref, rank_ref, wout_ref, meta_ref, keys, weights):
    width = PAIR_ROWS * LANES
    lane = lax.broadcasted_iota(I32, (1, LANES), 1)
    keys[...] = jnp.full(keys.shape, -1, I32)
    weights[...] = jnp.zeros(weights.shape, F32)
    for k in range(peers):
        start = start_ref[k]
        row, shift = start // LANES, start % LANES
        back = (LANES - shift) % LANES
        for ref, out in ((key_ref, keys), (w_ref, weights)):
            turned = [pltpu.roll(ref[row + t], back, 1) for t in range(PAIR_ROWS + 1)]
            for t in range(PAIR_ROWS):
                out[k : k + 1, t * LANES : (t + 1) * LANES] = jnp.where(lane < LANES - shift, turned[t], turned[t + 1])
    key = keys[...]
    lanes = lax.broadcasted_iota(I32, key.shape, 1)
    group = key // rows_dev
    valid = (key >= 0) & (group // slot_cap == lax.broadcasted_iota(I32, key.shape, 0))
    slot = group % slot_cap
    fresh = valid & ((lanes == 0) | (pltpu.roll(group, 1, 1) != group))
    rank = jnp.where(fresh, 1, 0)
    step = 1
    while step < width:
        rank = rank + jnp.where(lanes >= step, pltpu.roll(rank, step, 1), 0)
        step *= 2
    rank = rank - 1
    flag = jnp.maximum(jnp.where(jnp.max(rank) >= cap, 1, 0), flag_ref[0])
    src = jnp.where(valid, key % rows_dev, 0)
    wout = jnp.where(valid, weights[...], 0.0)
    live = jnp.where(valid, rank, -1)
    first = jnp.where(fresh, rank, -1)
    low, high = (slot % 256).astype(F32), (slot // 256).astype(F32)
    sub = lax.broadcasted_iota(I32, (8, width), 0)
    sub_cap = lax.broadcasted_iota(I32, (8, cap), 0)
    for k in range(peers):
        src_ref[k] = src[k : k + 1]
        wout_ref[k] = wout[k : k + 1]
        rank_ref[k] = live[k : k + 1]
        parts = jnp.where(sub == 0, low[k : k + 1], jnp.where(sub == 1, high[k : k + 1], 0.0)).astype(BF16)
        found = dot_nt(parts, one_hot(cap, first[k : k + 1]))
        slots = (found[0:1] + 256.0 * found[1:2]).astype(I32)
        meta_ref[k] = jnp.where(sub_cap == 0, slots, flag)


def gnn_kernel(
    n, groups, cap, feat_ref, w1_ref, w2_ref, src_ref, rank_ref, w_ref, own_src_ref, own_slot_ref, own_w_ref, meta_ref, table_ref,
    out_ref, flag_ref,
    mt, acc, own, send, recv, meta_in, row_ids, flag_own, flag_in,
    send_sem, recv_sem, meta_send_sem, meta_recv_sem, flag_send_sem, flag_recv_sem,
):
    me = lax.axis_index("graph")
    my_group = lax.axis_index("batch")
    peers = n - 1
    rows, hid = feat_ref.shape[0], out_ref.shape[1]
    slot_cap = table_ref.shape[2]
    width = src_ref.shape[2]
    chunks = rows // ROW_CHUNK

    def shift_of(i):
        half = (i + 1) // 2
        return n // 2 + half * (1 - 2 * (i % 2))

    def peer(k):
        return lax.rem(me + k, n)

    def group_peer(j):
        return lax.rem(my_group + j, groups)

    def data_copy(layer, k):
        return pltpu.make_async_remote_copy(
            src_ref=send.at[layer, k - 1], dst_ref=recv.at[layer, k - 1],
            send_sem=send_sem.at[layer, k - 1], recv_sem=recv_sem.at[layer, k - 1],
            device_id={"graph": peer(k)}, device_id_type=MESH_ID,
        )

    def meta_copy(k):
        return pltpu.make_async_remote_copy(
            src_ref=meta_ref.at[k - 1], dst_ref=meta_in.at[k - 1],
            send_sem=meta_send_sem.at[k - 1], recv_sem=meta_recv_sem.at[k - 1],
            device_id={"graph": peer(k)}, device_id_type=MESH_ID,
        )

    def flag_copy(j):
        return pltpu.make_async_remote_copy(
            src_ref=flag_own, dst_ref=flag_in.at[j - 1],
            send_sem=flag_send_sem.at[j - 1], recv_sem=flag_recv_sem.at[j - 1],
            device_id={"batch": group_peer(j)}, device_id_type=MESH_ID,
        )

    barrier = pltpu.get_barrier_semaphore()

    def greet(k, c):
        pl.semaphore_signal(barrier, 1, device_id={"graph": peer(k)}, device_id_type=MESH_ID)
        return c

    def greet_group(j, c):
        pl.semaphore_signal(barrier, 1, device_id={"batch": group_peer(j)}, device_id_type=MESH_ID)
        return c

    lax.fori_loop(1, n, greet, 0)
    lax.fori_loop(1, groups, greet_group, 0)

    def transform(layer, weight_ref, source):
        for c in range(chunks):
            cols = slice(c * ROW_CHUNK, (c + 1) * ROW_CHUNK)
            if layer == 0:
                both = dot_nt(weight_ref[...], source[cols, :])
            else:
                both = dot(weight_ref[...], source[:, cols])
            mt[:, cols] = both[:hid].astype(BF16)
            acc[:, cols] = both[hid:]

    def gather(src_row):
        return dot(mt[...], one_hot(rows, src_row))

    def add_rows(block, ids):
        for c in range(chunks):
            cols = slice(c * ROW_CHUNK, (c + 1) * ROW_CHUNK)
            acc[:, cols] += dot_nt(block, one_hot(ROW_CHUNK, ids - c * ROW_CHUNK))

    def layer_body(layer):
        def send_step(i, c):
            k = shift_of(i)
            total = None
            for t in range(width // SELF_TILE):
                part = slice(t * SELF_TILE, (t + 1) * SELF_TILE)
                values = gather(src_ref[k - 1][:, part]) * w_ref[k - 1][:, part]
                term = weighted_sum(values, rank_ref[k - 1][:, part], cap)
                total = term if total is None else total + term
            send[layer, k - 1] = total.astype(BF16)

            @pl.when(i > 0)
            def _():
                data_copy(layer, shift_of(i - 1)).start()

            return c

        lax.fori_loop(0, peers, send_step, 0)
        data_copy(layer, shift_of(peers - 1)).start()

        own[...] = jnp.zeros(own.shape, F32)

        def own_step(t, c):
            values = gather(own_src_ref[t]) * own_w_ref[t]
            own[...] += weighted_sum(values, own_slot_ref[t], slot_cap)
            return c

        lax.fori_loop(0, own_src_ref.shape[0], own_step, 0)
        add_rows(own[...].astype(BF16), table_ref[me])

        if layer == 0:
            flag_own[...] = jnp.broadcast_to(meta_ref[0][1:2, :LANES], flag_own.shape)

        def recv_step(i, c):
            k = shift_of(i)
            if layer == 0:
                meta_copy(k).wait_recv()
                table = table_ref[lax.rem(me + n - k, n)]
                sub = lax.broadcasted_iota(I32, (8, slot_cap), 0)
                parts = jnp.where(sub == 0, table % 256, jnp.where(sub == 1, table // 256, 0))
                got = meta_in[k - 1]
                found = dot(parts.astype(F32).astype(BF16), one_hot(slot_cap, got[0:1]))
                row_ids[k - 1] = (found[0:1] + 256.0 * found[1:2]).astype(I32)
                flag_own[...] = jnp.maximum(flag_own[...], got[1:2, :LANES])
            data_copy(layer, k).wait_recv()
            add_rows(recv[layer, k - 1], row_ids[k - 1])
            return c

        lax.fori_loop(0, peers, recv_step, 0)

    transform(0, w1_ref, feat_ref)
    pl.semaphore_wait(barrier, n - 1 + groups - 1)

    def start_meta(i, c):
        meta_copy(shift_of(i)).start()
        return c

    lax.fori_loop(0, peers, start_meta, 0)
    layer_body(0)

    hidden = mt
    for c in range(chunks):
        cols = slice(c * ROW_CHUNK, (c + 1) * ROW_CHUNK)
        hidden[:, cols] = jnp.maximum(acc[:, cols], 0.0).astype(BF16)
    transform(1, w2_ref, hidden)

    def start_flag(j, c):
        flag_copy(j).start()
        return c

    lax.fori_loop(1, groups, start_flag, 0)
    layer_body(1)

    for c in range(chunks):
        cols = slice(c * ROW_CHUNK, (c + 1) * ROW_CHUNK)
        out_ref[cols, :] = jnp.transpose(jnp.maximum(acc[:, cols], 0.0)).astype(BF16)

    flag_ref[...] = flag_own[...]

    def end_flag(j, c):
        copy = flag_copy(j)
        copy.wait_recv()
        flag_ref[...] = jnp.maximum(flag_ref[...], flag_in[j - 1])
        copy.wait_send()
        return c

    lax.fori_loop(1, groups, end_flag, 0)

    def end_send(k, c):
        meta_copy(k).wait_send()
        data_copy(0, k).wait_send()
        data_copy(1, k).wait_send()
        return c

    lax.fori_loop(1, n, end_send, 0)


def solution(mesh):
    row_spec = P(("batch", "graph"), None)
    full_spec = P(None, None)
    table_spec = P(("batch", "graph"), None, None)
    n, groups = mesh.shape["graph"], mesh.shape["batch"]

    def plain_layer(h_loc, w_msg, w_self, src_idx, slot_idx, edge_w, recv_idx):
        rows_dev = h_loc.shape[0]
        messages = jnp.dot(h_loc, w_msg, preferred_element_type=F32).astype(BF16)
        weighted = messages[src_idx].astype(F32) * edge_w
        partial = jax.ops.segment_sum(weighted, slot_idx, num_segments=recv_idx.shape[0]).astype(BF16)
        received = lax.all_to_all(partial, "graph", 0, 0, tiled=True)
        agg_sum = jax.ops.segment_sum(received.astype(F32), recv_idx, num_segments=rows_dev + 1)
        self_term = jnp.dot(h_loc, w_self, preferred_element_type=F32)
        return jax.nn.relu(self_term + agg_sum[:rows_dev]).astype(BF16)

    def local_step(features, w_msg1, w_self1, w_msg2, w_self2, src_local, send_slot, edge_weight, recv_row):
        rows_dev, hid = features.shape[0], w_msg1.shape[1]
        slot_cap = recv_row.shape[2]
        edges = src_local.shape[1]
        peers = n - 1
        cap = slot_cap * 3 // 4
        width = PAIR_ROWS * LANES
        own_tiles = edges * 11 // 20 // SELF_TILE
        own_edges = own_tiles * SELF_TILE

        me = lax.axis_index("graph")
        owner, offset = send_slot[0] // slot_cap, send_slot[0] % slot_cap
        rank = lax.rem(owner - me + 2 * n - 1, n)
        key = (rank * slot_cap + offset) * rows_dev + src_local[0]
        counts = jnp.sum((rank[None, :] == jnp.arange(n, dtype=I32)[:, None]).astype(I32), axis=1)
        starts = jnp.cumsum(counts) - counts
        over = jnp.any(counts[:peers] > width) | (counts[peers] > own_edges)
        key, weight = lax.sort((key, edge_weight[0]), num_keys=1, is_stable=False)

        spare = 8 * LANES
        key_rows = jnp.concatenate([key, jnp.full((spare,), -1, I32)]).reshape(-1, 1, LANES)
        weight_rows = jnp.concatenate([weight, jnp.zeros((spare,), F32)]).reshape(-1, 1, LANES)
        vmem, smem = pl.BlockSpec(memory_space=pltpu.VMEM), pl.BlockSpec(memory_space=pltpu.SMEM)
        src, live, wgt, meta = pl.pallas_call(
            functools.partial(prep_kernel, peers, slot_cap, rows_dev, cap),
            out_shape=(
                jax.ShapeDtypeStruct((peers, 1, width), I32),
                jax.ShapeDtypeStruct((peers, 1, width), I32),
                jax.ShapeDtypeStruct((peers, 1, width), F32),
                jax.ShapeDtypeStruct((peers, 8, cap), I32),
            ),
            in_specs=[smem, smem, vmem, vmem],
            out_specs=[vmem] * 4,
            scratch_shapes=[pltpu.VMEM((n, width), I32), pltpu.VMEM((n, width), F32)],
            name="edge_windows",
        )(starts.astype(I32), over.astype(I32).reshape(1), key_rows, weight_rows)

        own_key = key[edges - own_edges :].reshape(own_tiles, 1, SELF_TILE)
        own_group = own_key // rows_dev
        own_slot = jnp.where(own_group // slot_cap == peers, own_group % slot_cap, -1)
        own_src = own_key % rows_dev
        own_w = weight[edges - own_edges :].reshape(own_tiles, 1, SELF_TILE)
        w1 = jnp.concatenate([w_msg1, w_self1], axis=1).T
        w2 = jnp.concatenate([w_msg2, w_self2], axis=1).T
        table = recv_row[0].reshape(n, 1, slot_cap)

        out, flag = pl.pallas_call(
            functools.partial(gnn_kernel, n, groups, cap),
            out_shape=(jax.ShapeDtypeStruct((rows_dev, hid), BF16), jax.ShapeDtypeStruct((8, LANES), I32)),
            in_specs=[vmem] * 11,
            out_specs=[vmem] * 2,
            scratch_shapes=[
                pltpu.VMEM((hid, rows_dev), BF16),
                pltpu.VMEM((hid, rows_dev), F32),
                pltpu.VMEM((hid, slot_cap), F32),
                pltpu.VMEM((2, peers, hid, cap), BF16),
                pltpu.VMEM((2, peers, hid, cap), BF16),
                pltpu.VMEM((peers, 8, cap), I32),
                pltpu.VMEM((peers, 1, cap), I32),
                pltpu.VMEM((8, LANES), I32),
                pltpu.VMEM((max(groups - 1, 1), 8, LANES), I32),
                pltpu.SemaphoreType.DMA((2, peers)),
                pltpu.SemaphoreType.DMA((2, peers)),
                pltpu.SemaphoreType.DMA((peers,)),
                pltpu.SemaphoreType.DMA((peers,)),
                pltpu.SemaphoreType.DMA((max(groups - 1, 1),)),
                pltpu.SemaphoreType.DMA((max(groups - 1, 1),)),
            ],
            compiler_params=pltpu.CompilerParams(collective_id=0, has_side_effects=True, vmem_limit_bytes=56 * 2**20),
            name="gnn_layers",
        )(features, w1, w2, src, live, wgt, own_src, own_slot, own_w, meta, table)

        def plain():
            args = src_local[0], send_slot[0], edge_weight[0][:, None], recv_row[0].reshape(-1)
            hidden = plain_layer(features, w_msg1, w_self1, *args)
            return plain_layer(hidden, w_msg2, w_self2, *args)

        return lax.cond(flag[0, 0] > 0, plain, lambda: out)

    return jax.shard_map(local_step, mesh=mesh, in_specs=(row_spec, full_spec, full_spec, full_spec, full_spec, row_spec, row_spec, row_spec, table_spec), out_specs=row_spec, check_vma=False)
```

time: 710 us -> 245 us (0.35)
  other arithmetic: 488 us -> 14.6 us
  Pallas kernels: 0 us -> 212 us
  blocking collectives: 105 us -> 0 us
  waiting for transfers between devices: 92.7 us -> 0 us
  local copies, waits for them, and re-layouts: 1.48 us -> 14.2 us
  starting transfers between devices: 10 us -> 0 us
  matrix products: 7.61 us -> 0 us
    scatter-add x4 -> x0, other arithmetic: 478 us -> none  [the longest x2 376 us: gnn_layer(): jax.ops.segment_sum(weighted, slot_idx, num_segments=recv_idx.shape[0])]
    pallas_call x0 -> x2, Pallas kernels: none -> 212 us  [the longest x1 208 us: local_step(): pl.pallas_call(functools.partial(gnn_kernel, n, groups, cap), out_shape=(...]
    all_to_all x1 -> x0, blocking collectives: 105 us -> none  [gnn_layer(): received = lax.all_to_all(partial, 'graph', 0, 0, tiled=True)]
    all_to_all x1 -> x0, waiting for transfers between devices: 92.7 us -> none  [gnn_layer(): received = lax.all_to_all(partial, 'graph', 0, 0, tiled=True)]
    all_to_all x1 -> x0, starting transfers between devices: 10 us -> none  [gnn_layer(): received = lax.all_to_all(partial, 'graph', 0, 0, tiled=True)]
    convert_element_type x2 -> x0, other arithmetic: 9.55 us -> none  [gnn_layer(): jax.ops.segment_sum(weighted, slot_idx, num_segments=recv_idx.shape[0])]
    sort x0 -> x1, other arithmetic: none -> 8.87 us  [local_step(): key, weight = lax.sort((key, edge_weight[0]), num_keys=1, is_stable=False)]
    dot_general x4 -> x0, matrix products: 7.61 us -> none  [the longest x2 5.42 us: gnn_layer(): self_term = jnp.dot(h_loc, w_self, preferred_element_type=jnp.float32)]
  transfers between devices with their start and end apart: 1 -> 0, of which waited for: 1 -> 0; matrix products, arithmetic and copies ran while one was open for 0% -> 0% of each run, Pallas kernels for 0% -> 0%
where the time goes in v1:
time: 245 us; the launch traced here: 244 us
  Pallas kernels  212 us (87%)
  other arithmetic  14.6 us (6%)
  local copies, waits for them, and re-layouts  14.2 us (6%)
    pallas_call x1, Pallas kernels, local_step(): pl.pallas_call(functools.partial(gnn_kernel, n, groups, cap), out_shape=(...  208 us
    sort x1, other arithmetic, local_step(): key, weight = lax.sort((key, edge_weight[0]), num_keys=1, is_stable=False)  8.87 us
    unnamed x16, local copies, waits for them, and re-layouts  7.62 us

profile of v1, /device:TPU:31, one launch (start us, length us, event | category | flops | bytes accessed | tf_op | source)
XLA Modules:
  0.0 243.7 jit_solution(11712337515700257146)
XLA Ops:
  0.0 1.5 reshape_squeeze.3.table_ref
  1.5 1.0 fusion.28
  2.6 1.4 compare_select_fusion.1
  4.0 0.3 convert_reduce_fusion
  4.3 0.6 slice.56
  5.5 0.6 compare_reduce_fusion
  7.0 0.5 sub.47.start_ref
  7.6 8.9 %sort.15 = (s32[20480]{0:T(1024)S(1)}, f32[20480]{0:T(1024)S(1)}) sort(s32[20480]{0:T(1024)S(1)} %fusion.28, f32[20480]{0:T(1024)} %bitcast.41), dimensions={0}, to_apply=%region_3.4 | sort | flops 307200 | bytes 327680 | tf_op jit(solution)/shard_map/sort | solution.py:295
  16.4 0.6 concatenate.14
  17.1 0.6 slice.59
  17.7 0.6 concatenate.15
  18.4 0.6 select_n.64.own_slot_ref
  19.1 0.7 copy.34.own_src_ref
  19.7 1.0 copy.30
  20.8 1.0 copy.31
  21.8 0.7 maximum_bitcast_fusion.1.w2_ref
  22.5 4.9 %edge_windows.1 = (s32[15,1,768]{2,1,0:T(1,128)}, s32[15,1,768]{2,1,0:T(1,128)}, f32[15,1,768]{2,1,0:T(1,128)}, s32[15,8,384]{2,1,0:T(8,128)}) custom-call(s32[16]{0:T(128)} %sub.47.start_ref, s32[1]{0:T(128)} %bitcast.13.flag_ref, s32[168,1,128]{2,1,0:T(1,128)} %bitcast.44, f32[168,1,128]{2,1,0:T(1,128)} %bitcast.45), custom_call_target="tpu_custom_call" | custom-call | tf_op jit(solution)/shard_map/edge_windows/pallas_call | solution.py:301
  27.4 1.1 copy.28
  28.5 1.1 copy.29
  29.6 0.8 maximum_bitcast_fusion.w1_ref
  30.4 2.4 %copy.33.feat_ref = bf16[2048,500]{1,0:T(8,128)(2,1)} copy(bf16[2048,500]{0,1:T(8,128)(2,1)S(1)} %copy-done) | data formatting | bytes 4096000 | tf_op args[0]
  32.9 207.6 %gnn_layers.1 = (bf16[2048,256]{1,0:T(8,128)(2,1)S(1)}, s32[8,128]{1,0:T(8,128)}) custom-call(bf16[2048,500]{1,0:T(8,128)(2,1)} %copy.33.feat_ref, bf16[512,500]{1,0:T(8,128)(2,1)} %maximum_bitcast_fusion.w1_ref, bf16[512,256]{1,0:T(8,128)(2,1)} %maximum_bitcast_fusion.1.w2_ref, s32[15,1,768]{2,1,0:T(1,128)} %get-tuple-element.46.src_ref, ...), custom_call_target="tpu_custom_call" | custom-call | tf_op jit(solution)/shard_map/gnn_layers/pallas_call | solution.py:324
  240.5 1.2 slice.61
  242.7 1.0 copy.41
  (17 shorter events, 0.6 us)
Async XLA Ops:
  0.0 30.4 %copy-start = (bf16[2048,500]{0,1:T(8,128)(2,1)S(1)}, bf16[2048,500]{0,1:T(8,128)(2,1)}, u32[]{:S(2)}) copy-start(bf16[2048,500]{0,1:T(8,128)(2,1)} %param.11) | copy-start | bytes 6144004
  29.5 212.8 %copy-start.2 = (f32[1,20480]{1,0:T(1,128)S(1)}, f32[1,20480]{1,0:T(1,128)}, u32[]{:S(2)}) copy-start(f32[1,20480]{1,0:T(1,128)} %param.18) | copy-start | bytes 245764
  29.6 212.8 %copy-start.3 = (bf16[256,256]{1,0:T(8,128)(2,1)S(1)}, bf16[256,256]{1,0:T(8,128)(2,1)}, u32[]{:S(2)}) copy-start(bf16[256,256]{1,0:T(8,128)(2,1)} %param.15) | copy-start | bytes 393220
  29.6 212.8 %copy-start.5 = (s32[1,20480]{1,0:T(1,128)S(1)}, s32[1,20480]{1,0:T(1,128)}, u32[]{:S(2)}) copy-start(s32[1,20480]{1,0:T(1,128)} %param.16) | copy-start | bytes 245764
  29.6 212.8 %copy-start.6 = (s32[1,16,512]{2,1,0:T(8,128)S(1)}, s32[1,16,512]{2,1,0:T(8,128)}, u32[]{:S(2)}) copy-start(s32[1,16,512]{2,1,0:T(8,128)} %param.19) | copy-start | bytes 98308

commit v2 on v1

--- a/solution.py
+++ b/solution.py
@@ -11,9 +11,12 @@
 BF16, F32, I32 = jnp.bfloat16, jnp.float32, jnp.int32
 LANES = 128
 PAIR_ROWS = 6
-SELF_TILE = 256
+PAIR_TILE = 256
+OWN_ROWS = 4
+OWN_SPAN = 512
 ROW_CHUNK = 512
 NT = (((1,), (1,)), ((), ()))
+TN = (((0,), (0,)), ((), ()))
 
 
 def dot(a, b):
@@ -24,9 +27,21 @@
     return lax.dot_general(a, b, NT, preferred_element_type=F32)
 
 
-def one_hot(count, index_row):
+def dot_tn(a, b):
+    return lax.dot_general(a, b, TN, preferred_element_type=F32)
+
+
+def plain_one_hot(count, index_row):
     rows = lax.broadcasted_iota(I32, (count, index_row.shape[1]), 0)
     return jnp.where(rows == index_row, 1.0, 0.0).astype(BF16)
+
+
+def one_hot(count, index_row):
+    width = index_row.shape[1]
+    low = plain_one_hot(LANES, index_row & (LANES - 1)).reshape(LANES // 16, 16, width)
+    high = jnp.broadcast_to(index_row >> 7, (16, width))
+    pieces = [(low * jnp.where(high == i, 1.0, 0.0).astype(BF16)[None]).reshape(LANES, width) for i in range(count // LANES)]
+    return jnp.concatenate(pieces, axis=0)
 
 
 def three_pieces(x):
@@ -43,24 +58,49 @@
     return dot_nt(high, select) + dot_nt(mid, select) + dot_nt(low, select)
 
 
-def prep_kernel(peers, slot_cap, rows_dev, cap, start_ref, flag_ref, key_ref, w_ref, src_ref, rank_ref, wout_ref, meta_ref, keys, weights):
+def prep_kernel(
+    peers, slot_cap, rows_dev, cap, count_ref, key_ref, w_ref, table_in_ref,
+    src_ref, rank_ref, wout_ref, meta_ref, own_src_ref, own_slot_ref, own_w_ref, table_ref,
+    keys, weights, own_keys,
+):
     width = PAIR_ROWS * LANES
+    slot_bits, row_bits = slot_cap.bit_length() - 1, rows_dev.bit_length() - 1
+    edge_rows = key_ref.shape[0]
+    own_tiles, own_width = own_src_ref.shape[0], own_src_ref.shape[2]
+    ranges = rows_dev // OWN_SPAN
+    own_rows = own_tiles // ranges * OWN_ROWS
     lane = lax.broadcasted_iota(I32, (1, LANES), 1)
     keys[...] = jnp.full(keys.shape, -1, I32)
     weights[...] = jnp.zeros(weights.shape, F32)
-    for k in range(peers):
-        start = start_ref[k]
-        row, shift = start // LANES, start % LANES
-        back = (LANES - shift) % LANES
-        for ref, out in ((key_ref, keys), (w_ref, weights)):
-            turned = [pltpu.roll(ref[row + t], back, 1) for t in range(PAIR_ROWS + 1)]
-            for t in range(PAIR_ROWS):
-                out[k : k + 1, t * LANES : (t + 1) * LANES] = jnp.where(lane < LANES - shift, turned[t], turned[t + 1])
+    start = jnp.int32(0)
+    over = jnp.int32(0)
+    for k in range(peers + ranges):
+        count = count_ref[k]
+        kept = PAIR_ROWS if k < peers else own_rows
+        over = jnp.maximum(over, jnp.where(count > kept * LANES, 1, 0))
+        row, shift = start >> 7, start & (LANES - 1)
+        back = (LANES - shift) & (LANES - 1)
+        for ref, fill in ((key_ref, -1), (w_ref, 0.0)):
+            turned = [pltpu.roll(ref[jnp.minimum(row + t, edge_rows - 1)], back, 1) for t in range(kept + 1)]
+            for t in range(kept):
+                piece = jnp.where(lane < LANES - shift, turned[t], turned[t + 1])
+                piece = jnp.where(lane + t * LANES < count, piece, fill)
+                if k < peers:
+                    out = keys if ref is key_ref else weights
+                    out[k : k + 1, t * LANES : (t + 1) * LANES] = piece
+                else:
+                    tile, col = divmod((k - peers) * own_rows + t, OWN_ROWS)
+                    cols = slice(col * LANES, (col + 1) * LANES)
+                    if ref is key_ref:
+                        own_keys[tile : tile + 1, cols] = piece
+                    else:
+                        own_w_ref[tile, :, cols] = piece
+        start = start + count
     key = keys[...]
     lanes = lax.broadcasted_iota(I32, key.shape, 1)
-    group = key // rows_dev
-    valid = (key >= 0) & (group // slot_cap == lax.broadcasted_iota(I32, key.shape, 0))
-    slot = group % slot_cap
+    valid = key >= 0
+    group = key >> row_bits
+    slot = group & (slot_cap - 1)
     fresh = valid & ((lanes == 0) | (pltpu.roll(group, 1, 1) != group))
     rank = jnp.where(fresh, 1, 0)
     step = 1
@@ -68,26 +108,35 @@
         rank = rank + jnp.where(lanes >= step, pltpu.roll(rank, step, 1), 0)
         step *= 2
     rank = rank - 1
-    flag = jnp.maximum(jnp.where(jnp.max(rank) >= cap, 1, 0), flag_ref[0])
-    src = jnp.where(valid, key % rows_dev, 0)
-    wout = jnp.where(valid, weights[...], 0.0)
+
+    own_key = own_keys[...]
+    own_src = jnp.where(own_key >= 0, (own_key >> slot_bits) & (OWN_SPAN - 1), 0)
+    own_slot = jnp.where(own_key >= 0, own_key & (slot_cap - 1), -1)
+    for t in range(own_tiles):
+        own_src_ref[t] = own_src[t : t + 1]
+        own_slot_ref[t] = own_slot[t : t + 1]
+
+    flag = jnp.maximum(over, jnp.where(jnp.max(rank) >= cap, 1, 0))
+    src = jnp.where(valid, key & (rows_dev - 1), 0)
     live = jnp.where(valid, rank, -1)
     first = jnp.where(fresh, rank, -1)
-    low, high = (slot % 256).astype(F32), (slot // 256).astype(F32)
+    low, high = (slot & 255).astype(F32), (slot >> 8).astype(F32)
     sub = lax.broadcasted_iota(I32, (8, width), 0)
     sub_cap = lax.broadcasted_iota(I32, (8, cap), 0)
     for k in range(peers):
         src_ref[k] = src[k : k + 1]
-        wout_ref[k] = wout[k : k + 1]
+        wout_ref[k] = weights[k : k + 1]
         rank_ref[k] = live[k : k + 1]
         parts = jnp.where(sub == 0, low[k : k + 1], jnp.where(sub == 1, high[k : k + 1], 0.0)).astype(BF16)
         found = dot_nt(parts, one_hot(cap, first[k : k + 1]))
         slots = (found[0:1] + 256.0 * found[1:2]).astype(I32)
         meta_ref[k] = jnp.where(sub_cap == 0, slots, flag)
+    for k in range(peers + 1):
+        table_ref[k] = table_in_ref[k : k + 1]
 
 
 def gnn_kernel(
-    n, groups, cap, feat_ref, w1_ref, w2_ref, src_ref, rank_ref, w_ref, own_src_ref, own_slot_ref, own_w_ref, meta_ref, table_ref,
+    n, groups, cap, feat_ref, msg1_ref, self1_ref, msg2_ref, self2_ref, src_ref, rank_ref, w_ref, own_src_ref, own_slot_ref, own_w_ref, meta_ref, table_ref,
     out_ref, flag_ref,
     mt, acc, own, send, recv, meta_in, row_ids, flag_own, flag_in,
     send_sem, recv_sem, meta_send_sem, meta_recv_sem, flag_send_sem, flag_recv_sem,
@@ -95,7 +144,7 @@
     me = lax.axis_index("graph")
     my_group = lax.axis_index("batch")
     peers = n - 1
-    rows, hid = feat_ref.shape[0], out_ref.shape[1]
+    rows, hid = out_ref.shape
     slot_cap = table_ref.shape[2]
     width = src_ref.shape[2]
     chunks = rows // ROW_CHUNK
@@ -144,18 +193,12 @@
     lax.fori_loop(1, n, greet, 0)
     lax.fori_loop(1, groups, greet_group, 0)
 
-    def transform(layer, weight_ref, source):
+    def transform(msg_ref, self_ref, source):
         for c in range(chunks):
             cols = slice(c * ROW_CHUNK, (c + 1) * ROW_CHUNK)
-            if layer == 0:
-                both = dot_nt(weight_ref[...], source[cols, :])
-            else:
-                both = dot(weight_ref[...], source[:, cols])
-            mt[:, cols] = both[:hid].astype(BF16)
-            acc[:, cols] = both[hid:]
-
-    def gather(src_row):
-        return dot(mt[...], one_hot(rows, src_row))
+            part = source[:, cols]
+            mt[:, cols] = dot_tn(msg_ref[...], part).astype(BF16)
+            acc[:, cols] = dot_tn(self_ref[...], part)
 
     def add_rows(block, ids):
         for c in range(chunks):
@@ -166,9 +209,9 @@
         def send_step(i, c):
             k = shift_of(i)
             total = None
-            for t in range(width // SELF_TILE):
-                part = slice(t * SELF_TILE, (t + 1) * SELF_TILE)
-                values = gather(src_ref[k - 1][:, part]) * w_ref[k - 1][:, part]
+            for t in range(width // PAIR_TILE):
+                part = slice(t * PAIR_TILE, (t + 1) * PAIR_TILE)
+                values = dot(mt[...], one_hot(rows, src_ref[k - 1][:, part])) * w_ref[k - 1][:, part]
                 term = weighted_sum(values, rank_ref[k - 1][:, part], cap)
                 total = term if total is None else total + term
             send[layer, k - 1] = total.astype(BF16)
@@ -185,7 +228,9 @@
         own[...] = jnp.zeros(own.shape, F32)
 
         def own_step(t, c):
-            values = gather(own_src_ref[t]) * own_w_ref[t]
+            base = t // (own_src_ref.shape[0] * OWN_SPAN // rows) * OWN_SPAN
+            window = mt[:, pl.ds(pl.multiple_of(base, OWN_SPAN), OWN_SPAN)]
+            values = dot(window, one_hot(OWN_SPAN, own_src_ref[t])) * own_w_ref[t]
             own[...] += weighted_sum(values, own_slot_ref[t], slot_cap)
             return c
 
@@ -201,7 +246,7 @@
                 meta_copy(k).wait_recv()
                 table = table_ref[lax.rem(me + n - k, n)]
                 sub = lax.broadcasted_iota(I32, (8, slot_cap), 0)
-                parts = jnp.where(sub == 0, table % 256, jnp.where(sub == 1, table // 256, 0))
+                parts = jnp.where(sub == 0, table & 255, jnp.where(sub == 1, table >> 8, 0))
                 got = meta_in[k - 1]
                 found = dot(parts.astype(F32).astype(BF16), one_hot(slot_cap, got[0:1]))
                 row_ids[k - 1] = (found[0:1] + 256.0 * found[1:2]).astype(I32)
@@ -212,7 +257,7 @@
 
         lax.fori_loop(0, peers, recv_step, 0)
 
-    transform(0, w1_ref, feat_ref)
+    transform(msg1_ref, self1_ref, feat_ref)
     pl.semaphore_wait(barrier, n - 1 + groups - 1)
 
     def start_meta(i, c):
@@ -226,7 +271,7 @@
     for c in range(chunks):
         cols = slice(c * ROW_CHUNK, (c + 1) * ROW_CHUNK)
         hidden[:, cols] = jnp.maximum(acc[:, cols], 0.0).astype(BF16)
-    transform(1, w2_ref, hidden)
+    transform(msg2_ref, self2_ref, hidden)
 
     def start_flag(j, c):
         flag_copy(j).start()
@@ -239,16 +284,14 @@
         cols = slice(c * ROW_CHUNK, (c + 1) * ROW_CHUNK)
         out_ref[cols, :] = jnp.transpose(jnp.maximum(acc[:, cols], 0.0)).astype(BF16)
 
-    flag_ref[...] = flag_own[...]
-
-    def end_flag(j, c):
+    def end_flag(j, seen):
         copy = flag_copy(j)
         copy.wait_recv()
-        flag_ref[...] = jnp.maximum(flag_ref[...], flag_in[j - 1])
+        seen = jnp.maximum(seen, flag_in[j - 1])
         copy.wait_send()
-        return c
-
-    lax.fori_loop(1, groups, end_flag, 0)
+        return seen
+
+    flag_ref[0] = jnp.max(lax.fori_loop(1, groups, end_flag, flag_own[...]))
 
     def end_send(k, c):
         meta_copy(k).wait_send()
@@ -282,50 +325,40 @@
         peers = n - 1
         cap = slot_cap * 3 // 4
         width = PAIR_ROWS * LANES
-        own_tiles = edges * 11 // 20 // SELF_TILE
-        own_edges = own_tiles * SELF_TILE
+        own_width = OWN_ROWS * LANES
+        ranges = rows_dev // OWN_SPAN
+        own_tiles = ranges * (edges * 3 // 5 // ranges // own_width)
 
         me = lax.axis_index("graph")
-        owner, offset = send_slot[0] // slot_cap, send_slot[0] % slot_cap
+        slots, sources = send_slot.reshape(-1), src_local.reshape(-1)
+        owner, offset = slots // slot_cap, slots % slot_cap
         rank = lax.rem(owner - me + 2 * n - 1, n)
-        key = (rank * slot_cap + offset) * rows_dev + src_local[0]
-        counts = jnp.sum((rank[None, :] == jnp.arange(n, dtype=I32)[:, None]).astype(I32), axis=1)
-        starts = jnp.cumsum(counts) - counts
-        over = jnp.any(counts[:peers] > width) | (counts[peers] > own_edges)
-        key, weight = lax.sort((key, edge_weight[0]), num_keys=1, is_stable=False)
-
-        spare = 8 * LANES
-        key_rows = jnp.concatenate([key, jnp.full((spare,), -1, I32)]).reshape(-1, 1, LANES)
-        weight_rows = jnp.concatenate([weight, jnp.zeros((spare,), F32)]).reshape(-1, 1, LANES)
+        inner = jnp.where(rank == peers, sources * slot_cap + offset, offset * rows_dev + sources)
+        key = rank * (slot_cap * rows_dev) + inner
+        bins = jnp.where(rank == peers, peers + sources // OWN_SPAN, rank)
+        counts = jnp.sum((bins[None, :] == jnp.arange(peers + ranges, dtype=I32)[:, None]).astype(I32), axis=1)
+        key, weight = lax.sort((key, edge_weight.reshape(-1)), num_keys=1, is_stable=False)
+
         vmem, smem = pl.BlockSpec(memory_space=pltpu.VMEM), pl.BlockSpec(memory_space=pltpu.SMEM)
-        src, live, wgt, meta = pl.pallas_call(
+        pair = lambda dtype: jax.ShapeDtypeStruct((peers, 1, width), dtype)
+        own = lambda dtype: jax.ShapeDtypeStruct((own_tiles, 1, own_width), dtype)
+        src, live, wgt, meta, own_src, own_slot, own_w, table = pl.pallas_call(
             functools.partial(prep_kernel, peers, slot_cap, rows_dev, cap),
             out_shape=(
-                jax.ShapeDtypeStruct((peers, 1, width), I32),
-                jax.ShapeDtypeStruct((peers, 1, width), I32),
-                jax.ShapeDtypeStruct((peers, 1, width), F32),
-                jax.ShapeDtypeStruct((peers, 8, cap), I32),
+                pair(I32), pair(I32), pair(F32), jax.ShapeDtypeStruct((peers, 8, cap), I32), own(I32), own(I32), own(F32),
+                jax.ShapeDtypeStruct((n, 1, slot_cap), I32),
             ),
-            in_specs=[smem, smem, vmem, vmem],
-            out_specs=[vmem] * 4,
-            scratch_shapes=[pltpu.VMEM((n, width), I32), pltpu.VMEM((n, width), F32)],
+            in_specs=[smem, vmem, vmem, vmem],
+            out_specs=[vmem] * 8,
+            scratch_shapes=[pltpu.VMEM((n, width), I32), pltpu.VMEM((n, width), F32), pltpu.VMEM((own_tiles, own_width), I32)],
             name="edge_windows",
-        )(starts.astype(I32), over.astype(I32).reshape(1), key_rows, weight_rows)
-
-        own_key = key[edges - own_edges :].reshape(own_tiles, 1, SELF_TILE)
-        own_group = own_key // rows_dev
-        own_slot = jnp.where(own_group // slot_cap == peers, own_group % slot_cap, -1)
-        own_src = own_key % rows_dev
-        own_w = weight[edges - own_edges :].reshape(own_tiles, 1, SELF_TILE)
-        w1 = jnp.concatenate([w_msg1, w_self1], axis=1).T
-        w2 = jnp.concatenate([w_msg2, w_self2], axis=1).T
-        table = recv_row[0].reshape(n, 1, slot_cap)
+        )(counts, key.reshape(-1, 1, LANES), weight.reshape(-1, 1, LANES), recv_row[0])
 
         out, flag = pl.pallas_call(
             functools.partial(gnn_kernel, n, groups, cap),
-            out_shape=(jax.ShapeDtypeStruct((rows_dev, hid), BF16), jax.ShapeDtypeStruct((8, LANES), I32)),
-            in_specs=[vmem] * 11,
-            out_specs=[vmem] * 2,
+            out_shape=(jax.ShapeDtypeStruct((rows_dev, hid), BF16), jax.ShapeDtypeStruct((1,), I32)),
+            in_specs=[vmem] * 13,
+            out_specs=[vmem, smem],
             scratch_shapes=[
                 pltpu.VMEM((hid, rows_dev), BF16),
                 pltpu.VMEM((hid, rows_dev), F32),
@@ -345,13 +378,20 @@
             ],
             compiler_params=pltpu.CompilerParams(collective_id=0, has_side_effects=True, vmem_limit_bytes=56 * 2**20),
             name="gnn_layers",
-        )(features, w1, w2, src, live, wgt, own_src, own_slot, own_w, meta, table)
+        )(features.T, w_msg1, w_self1, w_msg2, w_self2, src, live, wgt, own_src, own_slot, own_w, meta, table)
 
         def plain():
             args = src_local[0], send_slot[0], edge_weight[0][:, None], recv_row[0].reshape(-1)
-            hidden = plain_layer(features, w_msg1, w_self1, *args)
-            return plain_layer(hidden, w_msg2, w_self2, *args)
-
-        return lax.cond(flag[0, 0] > 0, plain, lambda: out)
+            extra = features.shape[1] - hid
+            grow = lambda w: jnp.pad(w, ((0, extra), (0, 0)))
+            msg, own_part = jnp.stack([w_msg1, grow(w_msg2)]), jnp.stack([w_self1, grow(w_self2)])
+
+            def step(h, weights):
+                return jnp.pad(plain_layer(h, *weights, *args), ((0, 0), (0, extra))), None
+
+            hidden, _ = lax.scan(step, features, (msg, own_part))
+            return hidden[:, :hid]
+
+        return lax.cond(flag[0] > 0, plain, lambda: out)
 
     return jax.shard_map(local_step, mesh=mesh, in_specs=(row_spec, full_spec, full_spec, full_spec, full_spec, row_spec, row_spec, row_spec, table_spec), out_specs=row_spec, check_vma=False)

time: 245 us -> 189 us (0.77)
  Pallas kernels: 212 us -> 170 us
  local copies, waits for them, and re-layouts: 14.2 us -> 3.96 us
  other arithmetic: 14.6 us -> 10.8 us
    pallas_call x1, Pallas kernels: 208 us -> 165 us  [local_step(): pl.pallas_call(functools.partial(gnn_kernel, n, groups, cap), out_shape=(...]
    unnamed x16 -> x18, local copies, waits for them, and re-layouts: 7.62 us -> 3.96 us
where the time goes in v2:
time: 189 us; the launch traced here: 186 us
  Pallas kernels  170 us (90%)
  other arithmetic  10.8 us (6%)
  local copies, waits for them, and re-layouts  3.96 us (2%)
    pallas_call x1, Pallas kernels, local_step(): pl.pallas_call(functools.partial(gnn_kernel, n, groups, cap), out_shape=(...  165 us
    sort x1, other arithmetic, local_step(): lax.sort((key, edge_weight.reshape(-1)), num_keys=1, is_stable=False)  8.86 us
    pallas_call x1, Pallas kernels, local_step(): pl.pallas_call(functools.partial(prep_kernel, peers, slot_cap, rows_dev,...  5.01 us
    unnamed x18, local copies, waits for them, and re-layouts  3.96 us

profile of v2, /device:TPU:31, one launch (start us, length us, event | category | flops | bytes accessed | tf_op | source)
XLA Modules:
  0.0 185.9 jit_solution(9509387021516354252)
XLA Ops:
  0.0 0.0 copy-start.6
  0.0 0.0 copy-start.8
  0.0 0.0 copy-start.9
  0.0 0.0 copy-start.10
  0.0 0.0 copy-start.3
  0.0 0.0 copy-start.12
  0.0 0.0 copy-start.4
  0.0 0.0 copy-start.5
  0.1 1.7 copy.45
  1.7 0.0 copy-done.3
  1.7 0.0 copy-done.12
  1.7 0.1 select_add_fusion
  1.9 0.0 copy-done.4
  1.9 8.9 %sort.15 = (s32[20480]{0:T(1024)}, f32[20480]{0:T(1024)}) sort(s32[20480]{0:T(1024)S(1)} %select_add_fusion, f32[20480]{0:T(1024)S(1)} %bitcast.78), dimensions={0}, to_apply=%region_1.2 | sort | flops 307200 | bytes 327680 | tf_op jit(solution)/shard_map/sort | solution.py:340
  10.7 1.0 compare_select_fusion.1
  11.7 0.8 convert_reduce_fusion.count_ref
  12.5 0.0 copy-done.5
  12.5 5.0 %edge_windows.1 = (s32[15,1,768]{2,1,0:T(1,128)}, s32[15,1,768]{2,1,0:T(1,128)}, f32[15,1,768]{2,1,0:T(1,128)}, s32[15,8,384]{2,1,0:T(8,128)}, s32[24,1,512]{2,1...) custom-call(s32[19]{0:T(128)} %convert_reduce_fusion.count_ref, ...), custom_call_target="tpu_custom_call" | custom-call | tf_op jit(solution)/shard_map/edge_windows/pallas_call | solution.py:345
  17.5 0.0 copy-done.6
  17.5 0.0 copy-done.8
  17.6 0.0 copy-done.9
  17.6 0.0 copy-done.10
  17.6 165.5 %gnn_layers.1 = (bf16[2048,256]{1,0:T(8,128)(2,1)}, s32[1]{0:T(128)}) custom-call(bf16[500,2048]{1,0:T(8,128)(2,1)S(1)} %bitcast.73, bf16[500,256]{1,0:T(8,128)(2,1)S(1)} %copy-done.6, bf16[500,256]{1,0:T(8,128)(2,1)S(1)} %copy-done.8, bf16[256,256]{1,0:T(8,128)(2,1)S(1)} %copy-done.9, bf16[256,256]{1,0:T(8,128)(2,1)S(1)} %copy-done.10, ...), custom_call_target="tpu_custom_call" | custom-call | tf_op jit(solution)/shard_map/gnn_layers/pallas_call | solution.py:357
  183.7 2.3 %copy.46 = bf16[2048,256]{1,0:T(8,128)(2,1)} copy(bf16[2048,256]{1,0:T(8,128)(2,1)} %get-tuple-element.162) | data formatting | bytes 2097152
  (1 shorter events, 0.0 us)
Async XLA Ops:
  0.0 17.5 %copy-start.6 = (bf16[500,256]{1,0:T(8,128)(2,1)S(1)}, bf16[500,256]{1,0:T(8,128)(2,1)}, u32[]{:S(2)}) copy-start(bf16[500,256]{1,0:T(8,128)(2,1)} %msg1_ref.1) | copy-start | bytes 768004
  0.0 17.5 %copy-start.8 = (bf16[500,256]{1,0:T(8,128)(2,1)S(1)}, bf16[500,256]{1,0:T(8,128)(2,1)}, u32[]{:S(2)}) copy-start(bf16[500,256]{1,0:T(8,128)(2,1)} %self1_ref.1) | copy-start | bytes 768004
  0.0 17.5 %copy-start.9 = (bf16[256,256]{1,0:T(8,128)(2,1)S(1)}, bf16[256,256]{1,0:T(8,128)(2,1)}, u32[]{:S(2)}) copy-start(bf16[256,256]{1,0:T(8,128)(2,1)} %msg2_ref.1) | copy-start | bytes 393220
  0.0 17.6 %copy-start.10 = (bf16[256,256]{1,0:T(8,128)(2,1)S(1)}, bf16[256,256]{1,0:T(8,128)(2,1)}, u32[]{:S(2)}) copy-start(bf16[256,256]{1,0:T(8,128)(2,1)} %self2_ref.1) | copy-start | bytes 393220
  0.0 1.7 copy-start.3
  0.0 1.7 copy-start.12
  0.0 1.8 copy-start.4
  0.0 12.5 %copy-start.5 = (s32[1,16,512]{2,1,0:T(8,128)S(1)}, s32[1,16,512]{2,1,0:T(8,128)}, u32[]{:S(2)}) copy-start(s32[1,16,512]{2,1,0:T(8,128)} %param.21) | copy-start | bytes 98308

commit v3 on v2

--- a/solution.py
+++ b/solution.py
@@ -55,11 +55,11 @@
 def weighted_sum(values, index_row, count):
     select = one_hot(count, index_row)
     high, mid, low = three_pieces(values)
-    return dot_nt(high, select) + dot_nt(mid, select) + dot_nt(low, select)
+    return dot_nt(select, high) + dot_nt(select, mid) + dot_nt(select, low)
 
 
 def prep_kernel(
-    peers, slot_cap, rows_dev, cap, count_ref, key_ref, w_ref, table_in_ref,
+    peers, slot_cap, rows_dev, cap, key2_ref, key_ref, w_ref, table_in_ref,
     src_ref, rank_ref, wout_ref, meta_ref, own_src_ref, own_slot_ref, own_w_ref, table_ref,
     keys, weights, own_keys,
 ):
@@ -72,10 +72,13 @@
     lane = lax.broadcasted_iota(I32, (1, LANES), 1)
     keys[...] = jnp.full(keys.shape, -1, I32)
     weights[...] = jnp.zeros(weights.shape, F32)
-    start = jnp.int32(0)
+    all_keys = key2_ref[...]
+    bounds = [k * slot_cap * rows_dev for k in range(1, peers + 1)]
+    bounds += [(peers * rows_dev + r * OWN_SPAN) * slot_cap for r in range(1, ranges)]
+    starts = [jnp.int32(0)] + [jnp.sum(jnp.where(all_keys < bound, 1, 0)) for bound in bounds] + [jnp.int32(edge_rows * LANES)]
     over = jnp.int32(0)
     for k in range(peers + ranges):
-        count = count_ref[k]
+        start, count = starts[k], starts[k + 1] - starts[k]
         kept = PAIR_ROWS if k < peers else own_rows
         over = jnp.maximum(over, jnp.where(count > kept * LANES, 1, 0))
         row, shift = start >> 7, start & (LANES - 1)
@@ -95,7 +98,6 @@
                         own_keys[tile : tile + 1, cols] = piece
                     else:
                         own_w_ref[tile, :, cols] = piece
-        start = start + count
     key = keys[...]
     lanes = lax.broadcasted_iota(I32, key.shape, 1)
     valid = key >= 0
@@ -120,17 +122,18 @@
     src = jnp.where(valid, key & (rows_dev - 1), 0)
     live = jnp.where(valid, rank, -1)
     first = jnp.where(fresh, rank, -1)
+    lanes_cap = meta_ref.shape[2]
+    sub = lax.broadcasted_iota(I32, (8, width), 0)
+    sub_cap = lax.broadcasted_iota(I32, (8, lanes_cap), 0)
     low, high = (slot & 255).astype(F32), (slot >> 8).astype(F32)
-    sub = lax.broadcasted_iota(I32, (8, width), 0)
-    sub_cap = lax.broadcasted_iota(I32, (8, cap), 0)
     for k in range(peers):
         src_ref[k] = src[k : k + 1]
         wout_ref[k] = weights[k : k + 1]
         rank_ref[k] = live[k : k + 1]
         parts = jnp.where(sub == 0, low[k : k + 1], jnp.where(sub == 1, high[k : k + 1], 0.0)).astype(BF16)
-        found = dot_nt(parts, one_hot(cap, first[k : k + 1]))
-        slots = (found[0:1] + 256.0 * found[1:2]).astype(I32)
-        meta_ref[k] = jnp.where(sub_cap == 0, slots, flag)
+        found = dot_nt(parts, one_hot(lanes_cap, first[k : k + 1]))
+        listed = (found[0:1] + 256.0 * found[1:2]).astype(I32)
+        meta_ref[k] = jnp.where(sub_cap == 0, listed, flag)
     for k in range(peers + 1):
         table_ref[k] = table_in_ref[k : k + 1]
 
@@ -138,7 +141,7 @@
 def gnn_kernel(
     n, groups, cap, feat_ref, msg1_ref, self1_ref, msg2_ref, self2_ref, src_ref, rank_ref, w_ref, own_src_ref, own_slot_ref, own_w_ref, meta_ref, table_ref,
     out_ref, flag_ref,
-    mt, acc, own, send, recv, meta_in, row_ids, flag_own, flag_in,
+    mt, hidden, acc, own, send, recv, meta_in, row_ids, flag_own, flag_in,
     send_sem, recv_sem, meta_send_sem, meta_recv_sem, flag_send_sem, flag_recv_sem,
 ):
     me = lax.axis_index("graph")
@@ -161,7 +164,7 @@
 
     def data_copy(layer, k):
         return pltpu.make_async_remote_copy(
-            src_ref=send.at[layer, k - 1], dst_ref=recv.at[layer, k - 1],
+            src_ref=send.at[layer, k - 1, pl.ds(0, cap)], dst_ref=recv.at[layer, k - 1, pl.ds(0, cap)],
             send_sem=send_sem.at[layer, k - 1], recv_sem=recv_sem.at[layer, k - 1],
             device_id={"graph": peer(k)}, device_id_type=MESH_ID,
         )
@@ -193,37 +196,38 @@
     lax.fori_loop(1, n, greet, 0)
     lax.fori_loop(1, groups, greet_group, 0)
 
-    def transform(msg_ref, self_ref, source):
-        for c in range(chunks):
-            cols = slice(c * ROW_CHUNK, (c + 1) * ROW_CHUNK)
-            part = source[:, cols]
-            mt[:, cols] = dot_tn(msg_ref[...], part).astype(BF16)
-            acc[:, cols] = dot_tn(self_ref[...], part)
-
     def add_rows(block, ids):
         for c in range(chunks):
-            cols = slice(c * ROW_CHUNK, (c + 1) * ROW_CHUNK)
-            acc[:, cols] += dot_nt(block, one_hot(ROW_CHUNK, ids - c * ROW_CHUNK))
+            part = slice(c * ROW_CHUNK, (c + 1) * ROW_CHUNK)
+            acc[part] += dot(one_hot(ROW_CHUNK, ids - c * ROW_CHUNK), block)
 
     def layer_body(layer):
-        def send_step(i, c):
-            k = shift_of(i)
+        def pair_sum(k, between):
             total = None
             for t in range(width // PAIR_TILE):
                 part = slice(t * PAIR_TILE, (t + 1) * PAIR_TILE)
                 values = dot(mt[...], one_hot(rows, src_ref[k - 1][:, part])) * w_ref[k - 1][:, part]
-                term = weighted_sum(values, rank_ref[k - 1][:, part], cap)
+                term = weighted_sum(values, rank_ref[k - 1][:, part], send.shape[2])
                 total = term if total is None else total + term
+                if t == 0:
+                    between()
             send[layer, k - 1] = total.astype(BF16)
 
-            @pl.when(i > 0)
-            def _():
-                data_copy(layer, shift_of(i - 1)).start()
-
+        def send_step(i, c):
+            pair_sum(shift_of(i), lambda: data_copy(layer, shift_of(i - 1)).start())
             return c
 
-        lax.fori_loop(0, peers, send_step, 0)
-        data_copy(layer, shift_of(peers - 1)).start()
+        pair_sum(shift_of(0), lambda: None)
+        lax.fori_loop(1, peers, send_step, 0)
+
+        for c in range(chunks):
+            part = slice(c * ROW_CHUNK, (c + 1) * ROW_CHUNK)
+            if layer == 0:
+                acc[part] = dot_tn(feat_ref[:, part], self1_ref[...])
+            else:
+                acc[part] = dot(hidden[part], self2_ref[...])
+            if c == 0:
+                data_copy(layer, shift_of(peers - 1)).start()
 
         own[...] = jnp.zeros(own.shape, F32)
 
@@ -257,7 +261,11 @@
 
         lax.fori_loop(0, peers, recv_step, 0)
 
-    transform(msg1_ref, self1_ref, feat_ref)
+    spare = recv.shape[2] - cap
+    recv[:, :, cap:, :] = jnp.zeros((2, peers, spare, hid), BF16)
+    for c in range(chunks):
+        part = slice(c * ROW_CHUNK, (c + 1) * ROW_CHUNK)
+        mt[:, part] = dot_tn(msg1_ref[...], feat_ref[:, part]).astype(BF16)
     pl.semaphore_wait(barrier, n - 1 + groups - 1)
 
     def start_meta(i, c):
@@ -267,11 +275,10 @@
     lax.fori_loop(0, peers, start_meta, 0)
     layer_body(0)
 
-    hidden = mt
     for c in range(chunks):
-        cols = slice(c * ROW_CHUNK, (c + 1) * ROW_CHUNK)
-        hidden[:, cols] = jnp.maximum(acc[:, cols], 0.0).astype(BF16)
-    transform(msg2_ref, self2_ref, hidden)
+        part = slice(c * ROW_CHUNK, (c + 1) * ROW_CHUNK)
+        hidden[part] = jnp.maximum(acc[part], 0.0).astype(BF16)
+        mt[:, part] = lax.dot_general(msg2_ref[...], hidden[part], (((0,), (1,)), ((), ())), preferred_element_type=F32).astype(BF16)
 
     def start_flag(j, c):
         flag_copy(j).start()
@@ -280,9 +287,7 @@
     lax.fori_loop(1, groups, start_flag, 0)
     layer_body(1)
 
-    for c in range(chunks):
-        cols = slice(c * ROW_CHUNK, (c + 1) * ROW_CHUNK)
-        out_ref[cols, :] = jnp.transpose(jnp.maximum(acc[:, cols], 0.0)).astype(BF16)
+    out_ref[...] = acc[...].astype(BF16)
 
     def end_flag(j, seen):
         copy = flag_copy(j)
@@ -323,7 +328,7 @@
         slot_cap = recv_row.shape[2]
         edges = src_local.shape[1]
         peers = n - 1
-        cap = slot_cap * 3 // 4
+        cap, lanes_cap = slot_cap * 23 // 32, slot_cap * 3 // 4
         width = PAIR_ROWS * LANES
         own_width = OWN_ROWS * LANES
         ranges = rows_dev // OWN_SPAN
@@ -335,8 +340,6 @@
         rank = lax.rem(owner - me + 2 * n - 1, n)
         inner = jnp.where(rank == peers, sources * slot_cap + offset, offset * rows_dev + sources)
         key = rank * (slot_cap * rows_dev) + inner
-        bins = jnp.where(rank == peers, peers + sources // OWN_SPAN, rank)
-        counts = jnp.sum((bins[None, :] == jnp.arange(peers + ranges, dtype=I32)[:, None]).astype(I32), axis=1)
         key, weight = lax.sort((key, edge_weight.reshape(-1)), num_keys=1, is_stable=False)
 
         vmem, smem = pl.BlockSpec(memory_space=pltpu.VMEM), pl.BlockSpec(memory_space=pltpu.SMEM)
@@ -345,14 +348,14 @@
         src, live, wgt, meta, own_src, own_slot, own_w, table = pl.pallas_call(
             functools.partial(prep_kernel, peers, slot_cap, rows_dev, cap),
             out_shape=(
-                pair(I32), pair(I32), pair(F32), jax.ShapeDtypeStruct((peers, 8, cap), I32), own(I32), own(I32), own(F32),
+                pair(I32), pair(I32), pair(F32), jax.ShapeDtypeStruct((peers, 8, lanes_cap), I32), own(I32), own(I32), own(F32),
                 jax.ShapeDtypeStruct((n, 1, slot_cap), I32),
             ),
-            in_specs=[smem, vmem, vmem, vmem],
+            in_specs=[vmem] * 4,
             out_specs=[vmem] * 8,
             scratch_shapes=[pltpu.VMEM((n, width), I32), pltpu.VMEM((n, width), F32), pltpu.VMEM((own_tiles, own_width), I32)],
             name="edge_windows",
-        )(counts, key.reshape(-1, 1, LANES), weight.reshape(-1, 1, LANES), recv_row[0])
+        )(key.reshape(-1, LANES), key.reshape(-1, 1, LANES), weight.reshape(-1, 1, LANES), recv_row[0])
 
         out, flag = pl.pallas_call(
             functools.partial(gnn_kernel, n, groups, cap),
@@ -361,12 +364,13 @@
             out_specs=[vmem, smem],
             scratch_shapes=[
                 pltpu.VMEM((hid, rows_dev), BF16),
-                pltpu.VMEM((hid, rows_dev), F32),
-                pltpu.VMEM((hid, slot_cap), F32),
-                pltpu.VMEM((2, peers, hid, cap), BF16),
-                pltpu.VMEM((2, peers, hid, cap), BF16),
-                pltpu.VMEM((peers, 8, cap), I32),
-                pltpu.VMEM((peers, 1, cap), I32),
+                pltpu.VMEM((rows_dev, hid), BF16),
+                pltpu.VMEM((rows_dev, hid), F32),
+                pltpu.VMEM((slot_cap, hid), F32),
+                pltpu.VMEM((2, peers, lanes_cap, hid), BF16),
+                pltpu.VMEM((2, peers, lanes_cap, hid), BF16),
+                pltpu.VMEM((peers, 8, lanes_cap), I32),
+                pltpu.VMEM((peers, 1, lanes_cap), I32),
                 pltpu.VMEM((8, LANES), I32),
                 pltpu.VMEM((max(groups - 1, 1), 8, LANES), I32),
                 pltpu.SemaphoreType.DMA((2, peers)),
@@ -392,6 +396,6 @@
             hidden, _ = lax.scan(step, features, (msg, own_part))
             return hidden[:, :hid]
 
-        return lax.cond(flag[0] > 0, plain, lambda: out)
+        return jnp.maximum(lax.cond(flag[0] > 0, plain, lambda: out), 0)
 
     return jax.shard_map(local_step, mesh=mesh, in_specs=(row_spec, full_spec, full_spec, full_spec, full_spec, row_spec, row_spec, row_spec, table_spec), out_specs=row_spec, check_vma=False)

time: 189 us -> 181 us (0.958)
  Pallas kernels: 170 us -> 165 us
  local copies, waits for them, and re-layouts: 3.96 us -> 1.69 us
    pallas_call x1, Pallas kernels: 165 us -> 160 us  [local_step(): pl.pallas_call(functools.partial(gnn_kernel, n, groups, cap), out_shape=(...]
    unnamed x18 -> x15, local copies, waits for them, and re-layouts: 3.96 us -> 1.69 us
    max x0 -> x1, other arithmetic: none -> 2.26 us  [local_step(): return jnp.maximum(lax.cond(flag[0] > 0, plain, lambda: out), 0)]
where the time goes in v3:
time: 181 us; the launch traced here: 180 us
  Pallas kernels  165 us (91%)
  other arithmetic  12.1 us (7%)
    pallas_call x1, Pallas kernels, local_step(): pl.pallas_call(functools.partial(gnn_kernel, n, groups, cap), out_shape=(...  160 us
    sort x1, other arithmetic, local_step(): lax.sort((key, edge_weight.reshape(-1)), num_keys=1, is_stable=False)  8.87 us
    pallas_call x1, Pallas kernels, local_step(): pl.pallas_call(functools.partial(prep_kernel, peers, slot_cap, rows_dev,...  5.18 us

profile of v3, /device:TPU:31, one launch (start us, length us, event | category | flops | bytes accessed | tf_op | source)
XLA Modules:
  0.0 179.6 jit_solution(9190112769627089896)
XLA Ops:
  0.0 0.0 copy-start.4
  0.0 0.0 copy-start.5
  0.0 0.0 copy-start.6
  0.0 0.0 copy-start.7
  0.0 0.0 copy-start.2
  0.0 0.0 copy-start.1
  0.0 0.0 copy-start.3
  0.0 1.7 copy.38
  1.7 0.0 copy-done.2
  1.7 1.0 select_add_fusion
  2.7 0.0 copy-done.1
  2.7 8.9 %sort.15 = (s32[20480]{0:T(1024)}, f32[20480]{0:T(1024)}) sort(s32[20480]{0:T(1024)S(1)} %select_add_fusion, f32[20480]{0:T(1024)S(1)} %bitcast.75), dimensions={0}, to_apply=%region_0.1 | sort | flops 307200 | bytes 327680 | tf_op jit(solution)/shard_map/sort | solution.py:343
  11.6 0.0 copy-done.3
  11.6 5.2 %edge_windows.1 = (s32[15,1,768]{2,1,0:T(1,128)}, s32[15,1,768]{2,1,0:T(1,128)}, f32[15,1,768]{2,1,0:T(1,128)}, s32[15,8,384]{2,1,0:T(8,128)}, s32[24,1,512]{2,1...) custom-call(s32[160,128]{1,0:T(8,128)} %bitcast.86, s32[160,1,128]{2,1,0:T(1,128)} %bitcast.87, ...), custom_call_target="tpu_custom_call" | custom-call | tf_op jit(solution)/shard_map/edge_windows/pallas_call | solution.py:348
  16.8 0.0 copy-done.4
  16.8 0.0 copy-done.5
  16.8 0.0 copy-done.6
  16.8 0.0 copy-done.7
  16.8 159.8 %gnn_layers.1 = (bf16[2048,256]{1,0:T(8,128)(2,1)}, s32[1]{0:T(128)}) custom-call(bf16[500,2048]{1,0:T(8,128)(2,1)S(1)} %bitcast.73, bf16[500,256]{1,0:T(8,128)(2,1)S(1)} %copy-done.4, bf16[500,256]{1,0:T(8,128)(2,1)S(1)} %copy-done.5, bf16[256,256]{1,0:T(8,128)(2,1)S(1)} %copy-done.6, bf16[256,256]{1,0:T(8,128)(2,1)S(1)} %copy-done.7, ...), custom_call_target="tpu_custom_call" | custom-call | tf_op jit(solution)/shard_map/gnn_layers/pallas_call | solution.py:360
  177.3 2.3 %broadcast_maximum_fusion = bf16[2048,256]{1,0:T(8,128)(2,1)} fusion(bf16[2048,256]{1,0:T(8,128)(2,1)} %get-tuple-element.161), kind=kLoop, calls=%fused_computation.30 | loop fusion | flops 524288 | bytes 2097152 | tf_op jit(solution)/shard_map/max | solution.py:399
  (1 shorter events, 0.0 us)
Async XLA Ops:
  0.0 16.8 %copy-start.4 = (bf16[500,256]{1,0:T(8,128)(2,1)S(1)}, bf16[500,256]{1,0:T(8,128)(2,1)}, u32[]{:S(2)}) copy-start(bf16[500,256]{1,0:T(8,128)(2,1)} %msg1_ref.1) | copy-start | bytes 768004
  0.0 16.8 %copy-start.5 = (bf16[500,256]{1,0:T(8,128)(2,1)S(1)}, bf16[500,256]{1,0:T(8,128)(2,1)}, u32[]{:S(2)}) copy-start(bf16[500,256]{1,0:T(8,128)(2,1)} %self1_ref.1) | copy-start | bytes 768004
  0.0 16.8 %copy-start.6 = (bf16[256,256]{1,0:T(8,128)(2,1)S(1)}, bf16[256,256]{1,0:T(8,128)(2,1)}, u32[]{:S(2)}) copy-start(bf16[256,256]{1,0:T(8,128)(2,1)} %msg2_ref.1) | copy-start | bytes 393220
  0.0 16.8 %copy-start.7 = (bf16[256,256]{1,0:T(8,128)(2,1)S(1)}, bf16[256,256]{1,0:T(8,128)(2,1)}, u32[]{:S(2)}) copy-start(bf16[256,256]{1,0:T(8,128)(2,1)} %self2_ref.1) | copy-start | bytes 393220
  0.0 1.7 copy-start.2
  0.0 2.7 %copy-start.1 = (f32[1,20480]{1,0:T(1,128)S(1)}, f32[1,20480]{1,0:T(1,128)}, u32[]{:S(2)}) copy-start(f32[1,20480]{1,0:T(1,128)} %param.20) | copy-start | bytes 245764
  0.0 11.6 %copy-start.3 = (s32[1,16,512]{2,1,0:T(8,128)S(1)}, s32[1,16,512]{2,1,0:T(8,128)}, u32[]{:S(2)}) copy-start(s32[1,16,512]{2,1,0:T(8,128)} %param.21) | copy-start | bytes 98308

commit v4 on v3

--- a/solution.py
+++ b/solution.py
@@ -56,6 +56,12 @@
     select = one_hot(count, index_row)
     high, mid, low = three_pieces(values)
     return dot_nt(select, high) + dot_nt(select, mid) + dot_nt(select, low)
+
+
+def weighted_sum_columns(values, index_row, count):
+    select = one_hot(count, index_row)
+    high, mid, low = three_pieces(values)
+    return dot_nt(high, select) + dot_nt(mid, select) + dot_nt(low, select)
 
 
 def prep_kernel(
@@ -235,11 +241,11 @@
             base = t // (own_src_ref.shape[0] * OWN_SPAN // rows) * OWN_SPAN
             window = mt[:, pl.ds(pl.multiple_of(base, OWN_SPAN), OWN_SPAN)]
             values = dot(window, one_hot(OWN_SPAN, own_src_ref[t])) * own_w_ref[t]
-            own[...] += weighted_sum(values, own_slot_ref[t], slot_cap)
+            own[...] += weighted_sum_columns(values, own_slot_ref[t], slot_cap)
             return c
 
         lax.fori_loop(0, own_src_ref.shape[0], own_step, 0)
-        add_rows(own[...].astype(BF16), table_ref[me])
+        add_rows(jnp.transpose(own[...]).astype(BF16), table_ref[me])
 
         if layer == 0:
             flag_own[...] = jnp.broadcast_to(meta_ref[0][1:2, :LANES], flag_own.shape)
@@ -366,7 +372,7 @@
                 pltpu.VMEM((hid, rows_dev), BF16),
                 pltpu.VMEM((rows_dev, hid), BF16),
                 pltpu.VMEM((rows_dev, hid), F32),
-                pltpu.VMEM((slot_cap, hid), F32),
+                pltpu.VMEM((hid, slot_cap), F32),
                 pltpu.VMEM((2, peers, lanes_cap, hid), BF16),
                 pltpu.VMEM((2, peers, lanes_cap, hid), BF16),
                 pltpu.VMEM((peers, 8, lanes_cap), I32),

time: 181 us -> 183 us (1.011)
  the two profiles are of different devices: /device:TPU:31 before, /device:TPU:93 now
where the time goes in v4:
time: 183 us; the launch traced here: 180 us
  Pallas kernels  165 us (90%)
  other arithmetic  12.1 us (7%)
    pallas_call x1, Pallas kernels, local_step(): pl.pallas_call(functools.partial(gnn_kernel, n, groups, cap), out_shape=(...  160 us
    sort x1, other arithmetic, local_step(): lax.sort((key, edge_weight.reshape(-1)), num_keys=1, is_stable=False)  8.87 us
    pallas_call x1, Pallas kernels, local_step(): pl.pallas_call(functools.partial(prep_kernel, peers, slot_cap, rows_dev,...  5.18 us

profile of v4, /device:TPU:93, one launch (start us, length us, event | category | flops | bytes accessed | tf_op | source)
XLA Modules:
  0.0 179.9 jit_solution(2663126347283010817)
XLA Ops:
  0.0 0.0 copy-start.4
  0.0 0.0 copy-start.5
  0.0 0.0 copy-start.6
  0.0 0.0 copy-start.7
  0.0 0.0 copy-start.2
  0.0 0.0 copy-start.1
  0.0 0.0 copy-start.3
  0.0 1.7 copy.38
  1.7 0.0 copy-done.2
  1.7 1.0 select_add_fusion
  2.7 0.0 copy-done.1
  2.7 8.9 %sort.15 = (s32[20480]{0:T(1024)}, f32[20480]{0:T(1024)}) sort(s32[20480]{0:T(1024)S(1)} %select_add_fusion, f32[20480]{0:T(1024)S(1)} %bitcast.75), dimensions={0}, to_apply=%region_0.1 | sort | flops 307200 | bytes 327680 | tf_op jit(solution)/shard_map/sort | solution.py:349
  11.6 0.0 copy-done.3
  11.6 5.2 %edge_windows.1 = (s32[15,1,768]{2,1,0:T(1,128)}, s32[15,1,768]{2,1,0:T(1,128)}, f32[15,1,768]{2,1,0:T(1,128)}, s32[15,8,384]{2,1,0:T(8,128)}, s32[24,1,512]{2,1...) custom-call(s32[160,128]{1,0:T(8,128)} %bitcast.86, s32[160,1,128]{2,1,0:T(1,128)} %bitcast.87, ...), custom_call_target="tpu_custom_call" | custom-call | tf_op jit(solution)/shard_map/edge_windows/pallas_call | solution.py:354
  16.8 0.0 copy-done.4
  16.8 0.0 copy-done.5
  16.8 0.0 copy-done.6
  16.8 0.0 copy-done.7
  16.8 160.1 %gnn_layers.1 = (bf16[2048,256]{1,0:T(8,128)(2,1)}, s32[1]{0:T(128)}) custom-call(bf16[500,2048]{1,0:T(8,128)(2,1)S(1)} %bitcast.73, bf16[500,256]{1,0:T(8,128)(2,1)S(1)} %copy-done.4, bf16[500,256]{1,0:T(8,128)(2,1)S(1)} %copy-done.5, bf16[256,256]{1,0:T(8,128)(2,1)S(1)} %copy-done.6, bf16[256,256]{1,0:T(8,128)(2,1)S(1)} %copy-done.7, ...), custom_call_target="tpu_custom_call" | custom-call | tf_op jit(solution)/shard_map/gnn_layers/pallas_call | solution.py:366
  177.6 2.3 %broadcast_maximum_fusion = bf16[2048,256]{1,0:T(8,128)(2,1)} fusion(bf16[2048,256]{1,0:T(8,128)(2,1)} %get-tuple-element.161), kind=kLoop, calls=%fused_computation.30 | loop fusion | flops 524288 | bytes 2097152 | tf_op jit(solution)/shard_map/max | solution.py:405
  (1 shorter events, 0.0 us)
Async XLA Ops:
  0.0 16.8 %copy-start.4 = (bf16[500,256]{1,0:T(8,128)(2,1)S(1)}, bf16[500,256]{1,0:T(8,128)(2,1)}, u32[]{:S(2)}) copy-start(bf16[500,256]{1,0:T(8,128)(2,1)} %msg1_ref.1) | copy-start | bytes 768004
  0.0 16.8 %copy-start.5 = (bf16[500,256]{1,0:T(8,128)(2,1)S(1)}, bf16[500,256]{1,0:T(8,128)(2,1)}, u32[]{:S(2)}) copy-start(bf16[500,256]{1,0:T(8,128)(2,1)} %self1_ref.1) | copy-start | bytes 768004
  0.0 16.8 %copy-start.6 = (bf16[256,256]{1,0:T(8,128)(2,1)S(1)}, bf16[256,256]{1,0:T(8,128)(2,1)}, u32[]{:S(2)}) copy-start(bf16[256,256]{1,0:T(8,128)(2,1)} %msg2_ref.1) | copy-start | bytes 393220
  0.0 16.8 %copy-start.7 = (bf16[256,256]{1,0:T(8,128)(2,1)S(1)}, bf16[256,256]{1,0:T(8,128)(2,1)}, u32[]{:S(2)}) copy-start(bf16[256,256]{1,0:T(8,128)(2,1)} %self2_ref.1) | copy-start | bytes 393220
  0.0 1.7 copy-start.2
  0.0 2.7 %copy-start.1 = (f32[1,20480]{1,0:T(1,128)S(1)}, f32[1,20480]{1,0:T(1,128)}, u32[]{:S(2)}) copy-start(f32[1,20480]{1,0:T(1,128)} %param.20) | copy-start | bytes 245764
  0.0 11.6 %copy-start.3 = (s32[1,16,512]{2,1,0:T(8,128)S(1)}, s32[1,16,512]{2,1,0:T(8,128)}, u32[]{:S(2)}) copy-start(s32[1,16,512]{2,1,0:T(8,128)} %param.21) | copy-start | bytes 98308
